TPU v7x, 128 devices: a whole 4x4x4 slice. The times are simulated.
128 devices in a mesh: sector: 16 (over y, x_lo, core), row: 8 (over z, x_hi).
Axes of the slice: x: 4 (x_hi: 2, x_lo: 2; x = x_hi * 2 + x_lo), y: 4, z: 4, core: 2. Of those that a mesh axis runs over, the one named last changes fastest.
Arguments:
- psi_sectors: bfloat16 [64, 16384, 256], P('sector', 'row'), may hold values from -1.25 to 1.25
- stiff_blocks: bfloat16 [128, 5, 128, 128], P('row'), as said below
- mass_blocks: bfloat16 [128, 5, 128, 128], P('row'), as said below
- harmonic_table: int32 [32], replicated, may hold values from 0 to 31, each once
Outputs:
- reduced_stiffness: float32 [32, 512, 512], P('sector', 'row')
- reduced_mass: float32 [32, 512, 512], P('sector', 'row')
Inputs may be any that keep to these rules, and one draw needn't show every extreme that they name: The stiffness is symmetric: stiff_blocks[i, 2 + d] is the transpose of stiff_blocks[i + d, 2 - d], and blocks whose column lies outside 0 to 127 are zero. `mass_blocks`: the mass is symmetric in the same way, and diagonally dominant with a positive diagonal, hence positive definite.
All inputs are finite; a program needn't handle non-finite values.
Results may differ from a plain program's by a relative error of at most 0.0049.
Values may be sent and summed in bfloat16 or wider, within the bound.
No kernel may reach another device: no remote copies, remote signals or barrier semaphores. Data moves between devices by JAX's collectives and lax.ppermute only.
A program may use at most 128 MiB of HBM per device.

v0:
```python
import math

import jax
import jax.numpy as jnp
from jax import lax
from jax.sharding import PartitionSpec as P

B = 128
REACH = 2


def items_in_groups(x, axis, split_dim, concat_dim, work, item_dim, out_dim):
    items = jax.tree.leaves(x)[0].shape[item_dim]
    count = 2 if items % 2 == 0 else 1
    done = []
    for k in range(count):
        group = jax.tree.map(
            lambda a: lax.slice_in_dim(
                a, k * (items // count), (k + 1) * (items // count), axis=item_dim
            ),
            x,
        )
        done.append(
            work(
                lax.all_to_all(
                    group, axis, split_axis=split_dim, concat_axis=concat_dim, tiled=True
                )
            )
        )
    return jax.tree.map(lambda *parts: jnp.concatenate(parts, axis=out_dim), *done)


def padded(block, sides, width):
    for axis, dim in sides:
        count = lax.axis_size(axis)
        forward = [(i, i + 1) for i in range(count - 1)]
        backward = [(target, source) for source, target in forward]
        low = lax.ppermute(
            lax.slice_in_dim(block, block.shape[dim] - width, None, axis=dim), axis, forward
        )
        high = lax.ppermute(lax.slice_in_dim(block, 0, width, axis=dim), axis, backward)
        block = jnp.concatenate([low, block, high], axis=dim)
    return block


def split_up(x, dim, devices):
    before, after = (x.shape[:dim], x.shape[dim + 1 :])
    return jnp.moveaxis(x.reshape(*before, devices, -1, *after), dim, 0)


def summed_on_arrival(x, axis, dim):
    devices = lax.axis_size(axis)
    blocks = lax.all_to_all(split_up(x, dim, devices), axis, 0, 0, tiled=True)
    return jnp.sum(blocks.astype(jnp.float32), axis=0)


def in_one_piece(arrays, axis, dim, along):
    widths = [a.shape[along] for a in arrays]
    both = jnp.concatenate(arrays, axis=along)
    out = summed_on_arrival(both, axis, dim)
    return tuple(jnp.split(out, [sum(widths[:k]) for k in range(1, len(widths))], axis=along))


def coefficients(harmonic_table, sectors_all):
    sector_ids = jnp.arange(sectors_all, dtype=jnp.int32)
    half_count = sectors_all // 2
    second_freq = jnp.where(harmonic_table == 0, half_count, harmonic_table)
    first_phase = harmonic_table[:, None] * sector_ids[None, :] % sectors_all
    second_phase = second_freq[:, None] * sector_ids[None, :] % sectors_all
    angle_unit = 2.0 * math.pi / sectors_all
    first_angle = first_phase.astype(jnp.float32) * angle_unit
    second_angle = second_phase.astype(jnp.float32) * angle_unit
    zero_pair = (harmonic_table == 0)[:, None]
    low_scale = math.sqrt(1.0 / sectors_all)
    high_scale = math.sqrt(2.0 / sectors_all)
    first_row = jnp.where(zero_pair, low_scale, high_scale) * jnp.cos(first_angle)
    second = jnp.where(
        zero_pair, low_scale * jnp.cos(second_angle), high_scale * jnp.sin(second_angle)
    )
    return jnp.stack([first_row, second], axis=1).reshape(2 * harmonic_table.shape[0], sectors_all)


def per_device(psi_sectors, stiff_blocks, mass_blocks, harmonic_table):
    sec_dev, rows_dev, mode_count = psi_sectors.shape
    sectors_all = sec_dev * lax.axis_size("sector")
    dft_table = coefficients(harmonic_table, sectors_all)
    margin = REACH * B

    def transform(arrived):
        combined = jnp.einsum(
            "cs,srm->crm", dft_table, arrived.astype(jnp.float32), precision=lax.Precision.HIGHEST
        )
        return combined.astype(jnp.bfloat16)

    def columns_back(arrived):
        return lax.all_to_all(transform(arrived), "sector", split_axis=0, concat_axis=2, tiled=True)

    harmonics = items_in_groups(psi_sectors, "sector", 2, 0, columns_back, 1, 1)
    extended = padded(harmonics, (("row", 1),), margin)
    block_rows = rows_dev // B
    blocks_ext = extended.reshape(sec_dev, block_rows + 2 * REACH, B, mode_count)
    gathered = jnp.stack(
        [blocks_ext[:, offset : offset + block_rows] for offset in range(2 * REACH + 1)], axis=2
    )
    slot_dev = sec_dev // 2

    def paired(field_data):
        split = field_data.reshape(slot_dev, 2, rows_dev, mode_count)
        return split.transpose(0, 2, 1, 3).reshape(slot_dev, rows_dev, 2 * mode_count)

    def project_band(blocks):
        images = jnp.einsum(
            "ijab,cijbm->ciam", blocks, gathered, preferred_element_type=jnp.float32
        )
        return paired(images.astype(jnp.bfloat16).reshape(sec_dev, rows_dev, mode_count))

    left_basis = paired(harmonics)
    stiff_terms = jnp.einsum(
        "sra,srb->sab", left_basis, project_band(stiff_blocks), preferred_element_type=jnp.float32
    )
    mass_terms = jnp.einsum(
        "sra,srb->sab", left_basis, project_band(mass_blocks), preferred_element_type=jnp.float32
    )
    reduced_stiffness, reduced_mass = in_one_piece(
        (stiff_terms.astype(jnp.bfloat16), mass_terms.astype(jnp.bfloat16)), "row", 1, 0
    )
    return (reduced_stiffness, reduced_mass)


def solution(mesh):
    placed = (P("sector", "row", None), P("row", None, None, None), P("row", None, None, None), P())
    return jax.shard_map(
        per_device,
        mesh=mesh,
        in_specs=placed,
        out_specs=(P("sector", "row", None), P("sector", "row", None)),
        check_vma=False,
    )
```

profile of v0, /device:TPU:2, one launch (start us, length us, event | category | flops | bytes accessed | tf_op | source)
XLA Modules:
  0.0 287.0 jit_solution(13453881405923402012)
XLA Ops:
  0.6 0.0 copy-start
  0.6 4.6 %fusion.24 = (bf16[4,1024,256]{2,1,0:T(8,128)(2,1)}, bf16[4,1024,256]{2,1,0:T(8,128)(2,1)}) fusion(bf16[4,2048,256]{2,1,0:T(8,128)(2,1)} %param.4), kind=kLoop, calls=%fused_computation.51 | loop fusion | bytes 8388608 | tf_op jit(solution)/shard_map/slice | solution.py:18
  5.2 4.6 %copy.147 = bf16[4,1024,256]{1,0,2:T(4,128)(2,1)} copy(bf16[4,1024,256]{2,1,0:T(8,128)(2,1)} %get-tuple-element.7) | data formatting | bytes 4194304
  9.8 5.9 %all-to-all-start = ((bf16[4,1024,256]{1,0,2:T(4,128)(2,1)}), bf16[4,1024,256]{1,0,2:T(4,128)(2,1)}, u32[]{:S(2)}, u32[]{:S(2)}) async-start(bf16[4,1024,256]{1,0,2:T(4,128)(2,1)} %copy.147), calls=%async_computation | async-start | bytes 4194304 | tf_op jit(solution)/shard_map/all_to_all | solution.py:25
  15.8 4.5 %copy.148 = bf16[4,1024,256]{1,0,2:T(4,128)(2,1)} copy(bf16[4,1024,256]{2,1,0:T(8,128)(2,1)} %get-tuple-element.8) | data formatting | bytes 4194304
  20.3 22.1 %all-to-all-done = bf16[4,1024,256]{1,0,2:T(4,128)(2,1)} async-done(((bf16[4,1024,256]{1,0,2:T(4,128)(2,1)}), bf16[4,1024,256]{1,0,2:T(4,128)(2,1)}, u32[]{:S(2)}, u32[]{:S(2)}) %all-to-all-start) | async-done | bytes 2097184 | tf_op jit(solution)/shard_map/all_to_all | solution.py:25
  42.5 5.5 %all-to-all-start.2 = ((bf16[4,1024,256]{1,0,2:T(4,128)(2,1)}), bf16[4,1024,256]{1,0,2:T(4,128)(2,1)}, u32[]{:S(2)}, u32[]{:S(2)}) async-start(bf16[4,1024,256]{1,0,2:T(4,128)(2,1)} %copy.148), calls=%async_computation.2 | async-start | bytes 4194304 | tf_op jit(solution)/shard_map/all_to_all | solution.py:25
  48.0 0.0 copy-done.10
  48.0 0.2 fusion.13
  48.3 2.2 copy.117
  50.5 3.0 %copy.118 = bf16[16,4,1024,16]{2,1,0,3:T(4,128)(2,1)} copy(bf16[16,4,1024,16]{2,3,0,1:T(8,128)(2,1)S(1)} %bitcast.103) | data formatting | bytes 4194304 | tf_op jit(solution)/shard_map/all_to_all | solution.py:25
  53.5 4.0 %all_to_all.58 = bf16[64,1024,16]{1,0,2:T(8,128)(2,1)} reshape(bf16[16,4,1024,16]{2,1,0,3:T(4,128)(2,1)} %copy.118) | data formatting | bytes 4194304 | tf_op jit(solution)/shard_map/all_to_all | solution.py:25
  57.5 3.4 %convolution_convert_fusion.1 = bf16[64,1024,16]{1,0,2:T(8,128)(2,1)S(1)} fusion(f32[64,64,1]{1,0,2:T(8,128)S(1)} %bitcast.110, bf16[64,1024,16]{1,0,2:T(8,128)(2,1)} %all_to_all.58), kind=kOutput, calls=%fused_computation.22 | convolution fusion | flops 806354944 | bytes 4210688 | tf_op jit(solution)/shard_map/cs,srm->crm/dot_general | solution.py:90
  60.8 2.5 copy.119
  63.3 11.4 %all-to-all-done.2 = bf16[4,1024,256]{1,0,2:T(4,128)(2,1)} async-done(((bf16[4,1024,256]{1,0,2:T(4,128)(2,1)}), bf16[4,1024,256]{1,0,2:T(4,128)(2,1)}, u32[]{:S(2)}, u32[]{:S(2)}) %all-to-all-start.2) | async-done | bytes 2097184 | tf_op jit(solution)/shard_map/all_to_all | solution.py:25
  74.7 5.5 %all-to-all-start.1 = ((bf16[64,1024,16]{1,2,0:T(8,128)(2,1)}), bf16[64,1024,16]{1,2,0:T(8,128)(2,1)}, u32[]{:S(2)}, u32[]{:S(2)}) async-start(bf16[64,1024,16]{1,2,0:T(8,128)(2,1)} %copy.119), calls=%async_computation.1 | async-start | bytes 4194304 | tf_op jit(solution)/shard_map/all_to_all | solution.py:96
  80.2 2.2 copy.122
  82.5 2.9 %copy.123 = bf16[16,4,1024,16]{2,1,0,3:T(4,128)(2,1)} copy(bf16[16,4,1024,16]{2,3,0,1:T(8,128)(2,1)S(1)} %bitcast.104) | data formatting | bytes 4194304 | tf_op jit(solution)/shard_map/all_to_all | solution.py:25
  85.4 4.0 %all_to_all.65 = bf16[64,1024,16]{1,0,2:T(8,128)(2,1)} reshape(bf16[16,4,1024,16]{2,1,0,3:T(4,128)(2,1)} %copy.123) | data formatting | bytes 4194304 | tf_op jit(solution)/shard_map/all_to_all | solution.py:25
  89.4 3.4 %convolution_convert_fusion = bf16[64,1024,16]{1,0,2:T(8,128)(2,1)S(1)} fusion(f32[64,64,1]{1,0,2:T(8,128)S(1)} %bitcast.111, bf16[64,1024,16]{1,0,2:T(8,128)(2,1)} %all_to_all.65), kind=kOutput, calls=%fused_computation.21 | convolution fusion | flops 806354944 | bytes 4210688 | tf_op jit(solution)/shard_map/cs,srm->crm/dot_general | solution.py:90
  92.7 2.5 copy.124
  95.2 11.8 %all-to-all-done.1 = bf16[64,1024,16]{1,2,0:T(8,128)(2,1)} async-done(((bf16[64,1024,16]{1,2,0:T(8,128)(2,1)}), bf16[64,1024,16]{1,2,0:T(8,128)(2,1)}, u32[]{:S(2)}, u32[]{:S(2)}) %all-to-all-start.1) | async-done | bytes 2097184 | tf_op jit(solution)/shard_map/all_to_all | solution.py:96
  107.0 5.5 %all-to-all-start.3 = ((bf16[64,1024,16]{1,2,0:T(8,128)(2,1)}), bf16[64,1024,16]{1,2,0:T(8,128)(2,1)}, u32[]{:S(2)}, u32[]{:S(2)}) async-start(bf16[64,1024,16]{1,2,0:T(8,128)(2,1)} %copy.124), calls=%async_computation.3 | async-start | bytes 4194304 | tf_op jit(solution)/shard_map/all_to_all | solution.py:96
  112.5 1.8 copy.120
  114.3 0.0 copy-start.2
  114.3 1.3 copy-done.2
  115.6 0.9 slice.37
  116.5 1.3 collective-permute-start.1
  117.8 21.5 %all-to-all-done.3 = bf16[64,1024,16]{1,2,0:T(8,128)(2,1)} async-done(((bf16[64,1024,16]{1,2,0:T(8,128)(2,1)}), bf16[64,1024,16]{1,2,0:T(8,128)(2,1)}, u32[]{:S(2)}, u32[]{:S(2)}) %all-to-all-start.3) | async-done | bytes 2097184 | tf_op jit(solution)/shard_map/all_to_all | solution.py:96
  139.3 2.0 copy.125
  141.3 0.1 slice.36
  141.4 4.1 %collective-permute-start = (bf16[4,256,256]{1,2,0:T(8,128)(2,1)S(1)}, bf16[4,256,256]{1,2,0:T(8,128)(2,1)S(1)}, u32[]{:S(2)}, u32[]{:S(2)}) collective-permute-start(bf16[4,256,256]{1,2,0:T(8,128)(2,1)S(1)} %slice.36), channel_id=1, source_target_pairs={{0,1},{1,2},{2,3},{3,4},{4,5},{5,6},{6,7},{8,9},{9,10},{10,11},{11... | collective-permute-start | bytes 1572872 | tf_op jit(solution)/shard_map/ppermute | solution.py:38
  145.5 0.0 copy-done.3
  145.5 2.5 pad_maximum_fusion.1
  147.9 3.3 %collective-permute-done.1 = bf16[4,256,256]{1,2,0:T(8,128)(2,1)S(1)} collective-permute-done((bf16[4,256,256]{1,2,0:T(8,128)(2,1)}, bf16[4,256,256]{1,2,0:T(8,128)(2,1)S(1)}, u32[]{:S(2)}, u32[]{:S(2)}) %collective-permute-start.1) | collective-permute-done | bytes 524320 | tf_op jit(solution)/shard_map/ppermute | solution.py:41
  151.2 5.7 %collective-permute-done = bf16[4,256,256]{1,2,0:T(8,128)(2,1)S(1)} collective-permute-done((bf16[4,256,256]{1,2,0:T(8,128)(2,1)S(1)}, bf16[4,256,256]{1,2,0:T(8,128)(2,1)S(1)}, u32[]{:S(2)}, u32[]{:S(2)}) %collective-permute-start) | collective-permute-done | bytes 524320 | tf_op jit(solution)/shard_map/ppermute | solution.py:38
  156.9 2.9 pad_maximum_fusion
  159.7 8.0 %copy.128 = bf16[4,2560,256]{2,1,0:T(8,128)(2,1)} copy(bf16[4,2560,256]{1,2,0:T(8,128)(2,1)} %pad_maximum_fusion) | data formatting | bytes 10485760 | tf_op jit(solution)/shard_map/concatenate | solution.py:42
  167.7 13.9 %fusion.23 = (bf16[4,16,128,256]{3,2,1,0:T(8,128)(2,1)S(1)}, bf16[4,16,128,256]{3,2,1,0:T(8,128)(2,1)}, bf16[4,16,128,256]{3,2,1,0:T(8,128)(2,1)}, bf16[4,16,128,256]{3,2,1,0:T(8,128)(2,1)}, bf16[4,16,128,256]{3,2,1,0:T(8,128)(2,1)}) fusion(bf16[4,20,128,256]{3,2,1,0:T(8,128)(2,1)} %bitcast.93), kind=kLoop, calls=%fused_computation.50 | loop fusion | bytes 41943040 | tf_op jit(solution)/shard_map/slice | solution.py:103
  181.6 4.9 %fusion.6 = bf16[4,16,5,128,256]{4,3,2,0,1:T(8,128)(2,1)} fusion(bf16[4,16,128,256]{3,2,1,0:T(8,128)(2,1)} %get-tuple-element.6), kind=kLoop, calls=%fused_computation.15 | loop fusion | bytes 8388608
  186.5 0.0 copy-done.6
  186.5 2.4 fusion.5
  188.9 1.3 copy-done.5
  190.2 2.4 fusion.4
  192.6 1.3 copy-done.4
  193.9 2.3 fusion.3
  196.2 2.6 fusion.2
  198.8 0.0 copy-done
  198.8 10.7 %fusion = bf16[4,16,128,256]{3,2,0,1:T(8,128)(2,1)} fusion(bf16[4,16,5,128,256]{4,3,2,0,1:T(8,128)(2,1)} %fusion.2, bf16[16,5,128,128]{3,2,1,0:T(8,128)(2,1)S(1)} %copy-done), kind=kOutput, calls=%fused_computation.3 | convolution fusion | flops 2686451712 | bytes 27787264 | tf_op jit(solution)/shard_map/ijab,cijbm->ciam/dot_general | solution.py:112
  209.5 8.9 %fusion.1 = bf16[4,16,128,256]{3,2,0,1:T(8,128)(2,1)S(1)} fusion(bf16[4,16,5,128,256]{4,3,2,0,1:T(8,128)(2,1)} %fusion.2, bf16[16,5,128,128]{3,2,1,0:T(8,128)(2,1)S(1)} %copy-done.7), kind=kOutput, calls=%fused_computation.4 | convolution fusion | flops 2686451712 | bytes 27787264 | tf_op jit(solution)/shard_map/ijab,cijbm->ciam/dot_general | solution.py:112
  218.4 2.3 copy.137
  220.7 6.3 %copy.138 = bf16[2,2048,2,256]{1,3,2,0:T(8,128)(2,1)} copy(bf16[2,2048,2,256]{3,1,2,0:T(8,128)(2,1)} %bitcast.100) | data formatting | bytes 8388608 | tf_op jit(solution)/shard_map/transpose | solution.py:109
  227.0 4.7 %copy.134 = bf16[4,16,128,256]{3,2,1,0:T(8,128)(2,1)} copy(bf16[4,16,128,256]{3,2,0,1:T(8,128)(2,1)} %fusion) | data formatting | bytes 8388608 | tf_op jit(solution)/shard_map/convert_element_type | solution.py:115
  231.7 6.3 %copy.135 = bf16[2,2048,2,256]{1,3,2,0:T(8,128)(2,1)} copy(bf16[2,2048,2,256]{3,1,2,0:T(8,128)(2,1)} %bitcast.101) | data formatting | bytes 8388608 | tf_op jit(solution)/shard_map/transpose | solution.py:109
  238.0 6.0 %convolution_convert_fusion.2 = bf16[2,512,512]{2,1,0:T(8,128)(2,1)S(1)} fusion(bf16[2,2048,512]{1,2,0:T(8,128)(2,1)} %bitcast.106, bf16[2,2048,512]{1,2,0:T(8,128)(2,1)} %bitcast.108), kind=kOutput, calls=%fused_computation.23 | convolution fusion | flops 2148007936 | bytes 9437184 | tf_op jit(solution)/shard_map/sra,srb->sab/dot_general | solution.py:121
  244.0 0.0 copy-done.8
  244.0 0.0 copy-done.9
  244.0 2.4 convolution_convert_fusion.3
  246.3 0.2 pad_maximum_fusion.2
  246.5 0.0 copy-start.1
  246.5 0.1 copy.170
  246.7 39.2 %all_to_all.77 = bf16[8,4,64,512]{3,2,1,0:T(8,128)(2,1)S(1)} all-to-all(bf16[8,4,64,512]{3,2,1,0:T(8,128)(2,1)S(1)} %bitcast.105), channel_id=1, replica_groups=mesh['sector'=16,'row'=8] {'row'}, dimensions={0} | all-to-all | bytes 4194304 | tf_op jit(solution)/shard_map/all_to_all | solution.py:53
  285.9 0.3 convert_reduce_fusion
  286.2 0.8 fusion.25
  (15 shorter events, 0.1 us)
Async XLA Ops:
  0.6 198.2 %copy-start = (bf16[16,5,128,128]{3,2,1,0:T(8,128)(2,1)S(1)}, bf16[16,5,128,128]{3,2,1,0:T(8,128)(2,1)}, u32[]{:S(2)}) copy-start(bf16[16,5,128,128]{3,2,1,0:T(8,128)(2,1)} %param.5) | copy-start | bytes 7864324
  9.8 32.7 %all-to-all-start = ((bf16[4,1024,256]{1,0,2:T(4,128)(2,1)}), bf16[4,1024,256]{1,0,2:T(4,128)(2,1)}, u32[]{:S(2)}, u32[]{:S(2)}) async-start(bf16[4,1024,256]{1,0,2:T(4,128)(2,1)} %copy.147), calls=%async_computation | async-start | bytes 4194304 | tf_op jit(solution)/shard_map/all_to_all | solution.py:25
  15.8 32.2 %copy-start.10 = (s32[32]{0:T(128)S(1)}, s32[32]{0:T(128)}, u32[]{:S(2)}) copy-start(s32[32]{0:T(128)} %param.7) | copy-start | bytes 388
  42.5 32.2 %all-to-all-start.2 = ((bf16[4,1024,256]{1,0,2:T(4,128)(2,1)}), bf16[4,1024,256]{1,0,2:T(4,128)(2,1)}, u32[]{:S(2)}, u32[]{:S(2)}) async-start(bf16[4,1024,256]{1,0,2:T(4,128)(2,1)} %copy.148), calls=%async_computation.2 | async-start | bytes 4194304 | tf_op jit(solution)/shard_map/all_to_all | solution.py:25
  74.7 32.3 %all-to-all-start.1 = ((bf16[64,1024,16]{1,2,0:T(8,128)(2,1)}), bf16[64,1024,16]{1,2,0:T(8,128)(2,1)}, u32[]{:S(2)}, u32[]{:S(2)}) async-start(bf16[64,1024,16]{1,2,0:T(8,128)(2,1)} %copy.119), calls=%async_computation.1 | async-start | bytes 4194304 | tf_op jit(solution)/shard_map/all_to_all | solution.py:96
  107.0 32.3 %all-to-all-start.3 = ((bf16[64,1024,16]{1,2,0:T(8,128)(2,1)}), bf16[64,1024,16]{1,2,0:T(8,128)(2,1)}, u32[]{:S(2)}, u32[]{:S(2)}) async-start(bf16[64,1024,16]{1,2,0:T(8,128)(2,1)} %copy.124), calls=%async_computation.3 | async-start | bytes 4194304 | tf_op jit(solution)/shard_map/all_to_all | solution.py:96
  114.3 1.3 copy-start.2
  116.5 34.7 %collective-permute-start.1 = (bf16[4,256,256]{1,2,0:T(8,128)(2,1)}, bf16[4,256,256]{1,2,0:T(8,128)(2,1)S(1)}, u32[]{:S(2)}, u32[]{:S(2)}) collective-permute-start(bf16[4,256,256]{1,2,0:T(8,128)(2,1)} %slice.37), channel_id=1, source_target_pairs={{1,0},{2,1},{3,2},{4,3},{5,4},{6,5},{7,6},{9,8},{10,9},{11,10},{12... | collective-permute-start | bytes 1572872 | tf_op jit(solution)/shard_map/ppermute | solution.py:41
  139.3 6.2 %copy-start.3 = (bf16[4,1024,16,16]{1,3,2,0:T(8,128)(2,1)S(1)}, bf16[4,1024,16,16]{1,3,2,0:T(8,128)(2,1)}, u32[]{:S(2)}) copy-start(bf16[4,1024,16,16]{1,3,2,0:T(8,128)(2,1)} %copy-done.2) | copy-start | bytes 6291460
  141.4 15.5 %collective-permute-start = (bf16[4,256,256]{1,2,0:T(8,128)(2,1)S(1)}, bf16[4,256,256]{1,2,0:T(8,128)(2,1)S(1)}, u32[]{:S(2)}, u32[]{:S(2)}) collective-permute-start(bf16[4,256,256]{1,2,0:T(8,128)(2,1)S(1)} %slice.36), channel_id=1, source_target_pairs={{0,1},{1,2},{2,3},{3,4},{4,5},{5,6},{6,7},{8,9},{9,10},{10,11},{11... | collective-permute-start | bytes 1572872 | tf_op jit(solution)/shard_map/ppermute | solution.py:38
  181.6 4.9 %copy-start.6 = (bf16[4,16,128,256]{3,2,1,0:T(8,128)(2,1)S(1)}, bf16[4,16,128,256]{3,2,1,0:T(8,128)(2,1)}, u32[]{:S(2)}) copy-start(bf16[4,16,128,256]{3,2,1,0:T(8,128)(2,1)} %get-tuple-element.5) | copy-start | bytes 12582916
  186.5 3.7 %copy-start.5 = (bf16[4,16,128,256]{3,2,1,0:T(8,128)(2,1)S(1)}, bf16[4,16,128,256]{3,2,1,0:T(8,128)(2,1)}, u32[]{:S(2)}) copy-start(bf16[4,16,128,256]{3,2,1,0:T(8,128)(2,1)} %get-tuple-element.4) | copy-start | bytes 12582916
  190.2 3.7 %copy-start.4 = (bf16[4,16,128,256]{3,2,1,0:T(8,128)(2,1)S(1)}, bf16[4,16,128,256]{3,2,1,0:T(8,128)(2,1)}, u32[]{:S(2)}) copy-start(bf16[4,16,128,256]{3,2,1,0:T(8,128)(2,1)} %get-tuple-element.3) | copy-start | bytes 12582916
  198.8 10.7 %copy-start.7 = (bf16[16,5,128,128]{3,2,1,0:T(8,128)(2,1)S(1)}, bf16[16,5,128,128]{3,2,1,0:T(8,128)(2,1)}, u32[]{:S(2)}) copy-start(bf16[16,5,128,128]{3,2,1,0:T(8,128)(2,1)} %param.6) | copy-start | bytes 7864324
  238.0 6.0 %copy-start.8 = (bf16[2,2,2048,256]{2,3,1,0:T(8,128)(2,1)S(1)}, bf16[2,2,2048,256]{2,3,1,0:T(8,128)(2,1)}, u32[]{:S(2)}) copy-start(bf16[2,2,2048,256]{2,3,1,0:T(8,128)(2,1)} %pad_maximum_fusion.1) | copy-start | bytes 12582916
  238.0 6.0 %copy-start.9 = (bf16[2,2048,2,256]{1,3,2,0:T(8,128)(2,1)S(1)}, bf16[2,2048,2,256]{1,3,2,0:T(8,128)(2,1)}, u32[]{:S(2)}) copy-start(bf16[2,2048,2,256]{1,3,2,0:T(8,128)(2,1)} %copy.135) | copy-start | bytes 12582916
  246.5 40.5 %copy-start.1 = (bf16[16,5,128,128]{3,2,1,0:T(8,128)(2,1)S(1)}, bf16[16,5,128,128]{3,2,1,0:T(8,128)(2,1)}, u32[]{:S(2)}) copy-start(bf16[16,5,128,128]{3,2,1,0:T(8,128)(2,1)} %param.5) | copy-start | bytes 7864324
where the time goes:
time: 289 us; the launch traced here: 287 us
  local copies, waits for them, and re-layouts  103 us (36%)
  waiting for transfers between devices  75.8 us (26%)
  blocking collectives  39.2 us (14%)
  matrix products  34.6 us (12%)
  starting transfers between devices  27.8 us (10%)
  other arithmetic  6.03 us (2%)
    all_to_all x1, blocking collectives, summed_on_arrival(): blocks = lax.all_to_all(split_up(x, dim, devices), axis, 0, 0, tiled=True)  39.2 us
    all_to_all x2, waiting for transfers between devices, items_in_groups(): lax.all_to_all(group, axis, split_axis=split_dim, concat_axis=concat_dim,...  33.5 us
    all_to_all x2, waiting for transfers between devices, columns_back(): lax.all_to_all(transform(arrived), 'sector', split_axis=0, concat_axis=2,...  33.3 us
    unnamed x28, local copies, waits for them, and re-layouts  25.1 us
    dot_general x2, matrix products, project_band(): jnp.einsum('ijab,cijbm->ciam', blocks, gathered, preferred_element_type=j...  19.6 us
    all_to_all x6, local copies, waits for them, and re-layouts, items_in_groups(): lax.all_to_all(group, axis, split_axis=split_dim, concat_axis=concat_dim,...  18.3 us
    slice x1, local copies, waits for them, and re-layouts, per_device(): blocks_ext[:, offset:offset + block_rows]  13.9 us
    transpose x2, local copies, waits for them, and re-layouts, paired(): split.transpose(0, 2, 1, 3).reshape(slot_dev, rows_dev, 2 * mode_count)  12.6 us
  transfers between devices with their start and end apart: 6, of which 6 were waited for; matrix products, arithmetic and copies ran while one was open for 12% of the time, Pallas kernels for 0%

commit v1 on v0

v1 whole, which is shorter than its diff:
```python
import math

import jax
import jax.numpy as jnp
from jax import lax
from jax.experimental import pallas as pl
from jax.experimental.pallas import tpu as pltpu
from jax.sharding import PartitionSpec as P

B = 128
REACH = 2
LANES = 256
STEP_ROWS = 16


def slot_of_harmonic(harmonic_table):
    slots = jnp.arange(harmonic_table.shape[0], dtype=jnp.int32)
    hit = harmonic_table[:, None] == slots[None, :]
    return jnp.sum(jnp.where(hit, slots[:, None], 0), axis=0)


def real_dft8(x):
    half = math.sqrt(0.5)
    s0, d0 = x[0] + x[4], x[0] - x[4]
    s1, d1 = x[2] + x[6], x[2] - x[6]
    s2, d2 = x[1] + x[5], x[1] - x[5]
    s3, d3 = x[3] + x[7], x[3] - x[7]
    e0, e2 = s0 + s1, s0 - s1
    o0, o2 = s2 + s3, s2 - s3
    t_re, t_im = (d2 - d3) * half, (d2 + d3) * half
    return [
        (e0 + o0, None),
        (d0 + t_re, d1 + t_im),
        (e2, o2),
        (d0 - t_re, t_im - d1),
        (e0 - o0, None),
    ]


def dft4(a, b, c, d):
    s0, d0 = (a[0] + c[0], a[1] + c[1]), (a[0] - c[0], a[1] - c[1])
    s1, d1 = (b[0] + d[0], b[1] + d[1]), (b[0] - d[0], b[1] - d[1])
    return [
        (s0[0] + s1[0], s0[1] + s1[1]),
        (d0[0] - d1[1], d0[1] + d1[0]),
        (s0[0] - s1[0], s0[1] - s1[1]),
        (d0[0] + d1[1], d0[1] - d1[0]),
    ]


def complex_dft8(z):
    half = math.sqrt(0.5)
    even = dft4(z[0], z[2], z[4], z[6])
    odd = dft4(z[1], z[3], z[5], z[7])
    turned = [
        odd[0],
        ((odd[1][0] - odd[1][1]) * half, (odd[1][0] + odd[1][1]) * half),
        (-odd[2][1], odd[2][0]),
        (-(odd[3][0] + odd[3][1]) * half, (odd[3][0] - odd[3][1]) * half),
    ]
    low = [(e[0] + t[0], e[1] + t[1]) for e, t in zip(even, turned)]
    high = [(e[0] - t[0], e[1] - t[1]) for e, t in zip(even, turned)]
    return low + high


def transform_kernel(slot_ref, x_ref, out_ref, mid_ref):
    sectors = 64
    scale = math.sqrt(2.0 / sectors)

    def put(p, re, im):
        at = 2 * slot_ref[p]
        return at, re, im

    for tile in range(STEP_ROWS // 8):
        rows = slice(8 * tile, 8 * tile + 8)

        def store(c, value):
            out_ref[c, rows, :] = value.astype(jnp.bfloat16)

        for s0 in range(8):
            x = []
            for s1 in range(8):
                s = 8 * s1 + s0
                x.append(x_ref[s // 4, s % 4, rows, :].astype(jnp.float32))
            y = real_dft8(x)
            mid_ref[tile, 0, s0] = y[0][0]
            mid_ref[tile, 1, s0] = y[4][0]
            for k1 in range(1, 4):
                mid_ref[tile, 2 * k1, s0] = y[k1][0]
                mid_ref[tile, 2 * k1 + 1, s0] = y[k1][1]
        y = real_dft8([mid_ref[tile, 0, s0] for s0 in range(8)])
        at = 2 * slot_ref[0]
        store(at, y[0][0] * math.sqrt(1.0 / sectors))
        store(at + 1, y[4][0] * math.sqrt(1.0 / sectors))
        for k2 in range(1, 4):
            at = 2 * slot_ref[8 * k2]
            store(at, y[k2][0] * scale)
            store(at + 1, y[k2][1] * scale)
        z = []
        for s0 in range(8):
            angle = 2.0 * math.pi * 4 * s0 / sectors
            value = mid_ref[tile, 1, s0]
            z.append((value * (scale * math.cos(angle)), value * (scale * math.sin(angle))))
        y = complex_dft8(z)
        for k2 in range(4):
            at = 2 * slot_ref[4 + 8 * k2]
            store(at, y[k2][0])
            store(at + 1, y[k2][1])
        for k1 in range(1, 4):
            z = []
            for s0 in range(8):
                angle = 2.0 * math.pi * k1 * s0 / sectors
                c, s = scale * math.cos(angle), scale * math.sin(angle)
                re, im = mid_ref[tile, 2 * k1, s0], mid_ref[tile, 2 * k1 + 1, s0]
                z.append((re * c, im * c) if s0 == 0 else (re * c - im * s, re * s + im * c))
            y = complex_dft8(z)
            for k2 in range(8):
                p = k1 + 8 * k2
                if p < 32:
                    at = 2 * slot_ref[p]
                    store(at, y[k2][0])
                    store(at + 1, y[k2][1])
                else:
                    at = 2 * slot_ref[64 - p]
                    store(at, y[k2][0])
                    store(at + 1, -y[k2][1])


def transform(slots, arrived):
    groups, per, rows, cols = arrived.shape
    spec = pltpu.PrefetchScalarGridSpec(
        num_scalar_prefetch=1,
        grid=(rows // STEP_ROWS,),
        in_specs=[pl.BlockSpec((groups, per, STEP_ROWS, cols), lambda i, s: (0, 0, i, 0))],
        out_specs=pl.BlockSpec((groups * per, STEP_ROWS, cols), lambda i, s: (0, i, 0)),
        scratch_shapes=[pltpu.VMEM((STEP_ROWS // 8, 8, 8, 8, cols), jnp.float32)],
    )
    return pl.pallas_call(
        transform_kernel,
        grid_spec=spec,
        out_shape=jax.ShapeDtypeStruct((groups * per, rows, cols), jnp.bfloat16),
        compiler_params=pltpu.CompilerParams(dimension_semantics=("arbitrary",)),
        cost_estimate=pl.CostEstimate(
            flops=700 * rows * cols, bytes_accessed=4 * groups * per * rows * cols, transcendentals=0
        ),
        name="transform",
    )(slots, arrived)


def project_kernel(h_ref, halo_ref, stiff_ref, mass_ref, out_ref, y_ref, pt_ref, u_ref):
    blocks = h_ref.shape[0]
    slots = h_ref.shape[1] // 2

    def window(refs_rows):
        return jnp.concatenate(refs_rows, axis=0)

    def band_row(i, h0, h1, h2):
        rows = pl.ds(i * B, B)
        lhs = jnp.concatenate(
            [
                jnp.concatenate([r[i, 2] * jnp.bfloat16(0.5), r[i, 3], r[i, 4]], axis=1)
                for r in (stiff_ref, mass_ref)
            ],
            axis=0,
        )
        for c in range(2 * slots):
            rhs = jnp.concatenate([h0[c], h1[c], h2[c]], axis=0)
            y = jnp.dot(lhs, rhs, preferred_element_type=jnp.float32).astype(jnp.bfloat16)
            slot, part = c // 2, c % 2
            lanes = slice(LANES * part, LANES * part + LANES)
            lanes_m = slice(LANES * (2 + part), LANES * (2 + part) + LANES)
            y_ref[slot, rows, lanes] = y[:B]
            y_ref[slot, rows, lanes_m] = y[B:]
            pt_ref[slot, i, LANES * part : LANES * part + LANES, :] = h0[c].T

    def body(i, carry):
        band_row(i, h_ref.at[i], h_ref.at[i + 1], h_ref.at[i + 2])
        return carry

    lax.fori_loop(0, blocks - 2, body, 0)
    band_row(blocks - 2, h_ref.at[blocks - 2], h_ref.at[blocks - 1], halo_ref.at[0])
    band_row(blocks - 1, h_ref.at[blocks - 1], halo_ref.at[0], halo_ref.at[1])

    for slot in range(slots):
        p_t = jnp.concatenate([pt_ref[slot, i] for i in range(blocks)], axis=1)
        for n in range(4):
            u_ref[slot, :, LANES * n : LANES * n + LANES] = jnp.dot(
                p_t, y_ref[slot, :, LANES * n : LANES * n + LANES], preferred_element_type=jnp.float32
            )
    strips = out_ref.shape[0]
    high = out_ref.shape[2]
    for kind in range(2):
        for slot in range(slots):
            base = 2 * LANES * kind
            for q in range(4):
                direct = u_ref[slot, B * q : B * q + B, base : base + 2 * LANES]
                mirror = u_ref[slot, :, base + B * q : base + B * q + B].T
                total = (direct + mirror).astype(jnp.bfloat16)
                for part in range(B // high):
                    out_ref[q * (B // high) + part, kind * slots + slot] = total[
                        part * high : (part + 1) * high
                    ]


def project(h, halo, stiff, mass, strips):
    blocks, comps, _, cols = h.shape
    slots = comps // 2
    wide = 2 * cols
    vmem = pl.BlockSpec(memory_space=pltpu.VMEM)
    return pl.pallas_call(
        project_kernel,
        in_specs=[vmem] * 4,
        out_specs=vmem,
        out_shape=jax.ShapeDtypeStruct((strips, 2 * slots, wide // strips, wide), jnp.bfloat16),
        scratch_shapes=[
            pltpu.VMEM((slots, blocks * B, 2 * wide), jnp.bfloat16),
            pltpu.VMEM((slots, blocks, wide, B), jnp.bfloat16),
            pltpu.VMEM((slots, wide, 2 * wide), jnp.float32),
        ],
        compiler_params=pltpu.CompilerParams(vmem_limit_bytes=48 * 1024 * 1024),
        cost_estimate=pl.CostEstimate(
            flops=slots * blocks * B * wide * (2 * 2 * 3 * B + 2 * 2 * wide),
            bytes_accessed=2 * (h.size + halo.size + stiff.size + mass.size),
            transcendentals=0,
        ),
        name="project",
    )(h, halo, stiff, mass)


def per_device(psi_sectors, stiff_blocks, mass_blocks, harmonic_table):
    sec_dev, rows_dev, cols = psi_sectors.shape
    sector_count = lax.axis_size("sector")
    row_count = lax.axis_size("row")
    blocks = rows_dev // B
    pieces = psi_sectors.reshape(sec_dev, sector_count, rows_dev // sector_count, cols)
    pieces = jnp.swapaxes(pieces, 0, 1)
    arrived = lax.all_to_all(pieces, "sector", 0, 0, tiled=True)
    components = transform(slot_of_harmonic(harmonic_table), arrived)
    outgoing = components.reshape(sector_count, sec_dev, rows_dev // sector_count, cols)
    h = lax.all_to_all(outgoing, "sector", 0, 0, tiled=True)
    h = h.reshape(sector_count, sec_dev, -1, B, cols)
    h = jnp.swapaxes(h, 1, 2).reshape(blocks, sec_dev, B, cols)
    backward = [(i + 1, i) for i in range(row_count - 1)]
    halo = lax.ppermute(h[:REACH], "row", backward)
    parts = project(h, halo, stiff_blocks, mass_blocks, row_count)
    arrived_parts = lax.all_to_all(parts, "row", 0, 0, tiled=True)
    total = jnp.sum(arrived_parts.astype(jnp.float32), axis=0)
    slots = sec_dev // 2
    return total[:slots], total[slots:]


def solution(mesh):
    placed = (P("sector", "row", None), P("row", None, None, None), P("row", None, None, None), P())
    return jax.shard_map(
        per_device,
        mesh=mesh,
        in_specs=placed,
        out_specs=(P("sector", "row", None), P("sector", "row", None)),
        check_vma=False,
    )
```

time: 289 us -> 192 us (0.66)
  local copies, waits for them, and re-layouts: 103 us -> 5.52 us
  blocking collectives: 39.2 us -> 89.5 us
  matrix products: 34.6 us -> 0 us
  Pallas kernels: 0 us -> 23.1 us
  starting transfers between devices: 27.8 us -> 7.37 us
  waiting for transfers between devices: 75.8 us -> 64.6 us
  other arithmetic: 6.03 us -> 0.9 us
    all_to_all x1 -> x2, blocking collectives: 39.2 us -> 89.5 us  [the longest x1 54.2 us: per_device(): h = lax.all_to_all(outgoing, 'sector', 0, 0, tiled=True)]
    dot_general x6 -> x0, matrix products: 34.6 us -> none  [the longest x2 19.6 us: project_band(): jnp.einsum('ijab,cijbm->ciam', blocks, gathered, preferred_element_type=j...]
    unnamed x28 -> x6, local copies, waits for them, and re-layouts: 25.1 us -> 0.01 us
    pallas_call x0 -> x2, Pallas kernels: none -> 23.1 us  [the longest x1 14.4 us: project(): pl.pallas_call(project_kernel, in_specs=[vmem] * 4, out_specs=vmem, out_s...]
    all_to_all x8 -> x0, local copies, waits for them, and re-layouts: 22.1 us -> none  [the longest x6 18.3 us: items_in_groups(): lax.all_to_all(group, axis, split_axis=split_dim, concat_axis=concat_dim,...]
    slice x4 -> x2, local copies, waits for them, and re-layouts: 19.4 us -> 0.86 us  [the longest x1 0.83 us: per_device(): return (total[:slots], total[slots:])]
    all_to_all x4 -> x1, waiting for transfers between devices: 66.8 us -> 48.6 us  [per_device(): arrived = lax.all_to_all(pieces, 'sector', 0, 0, tiled=True)]
    all_to_all x4 -> x1, starting transfers between devices: 22.5 us -> 6.08 us  [per_device(): arrived = lax.all_to_all(pieces, 'sector', 0, 0, tiled=True)]
  transfers between devices with their start and end apart: 6 -> 2, of which waited for: 6 -> 2; matrix products, arithmetic and copies ran while one was open for 12% -> 0% of each run, Pallas kernels for 0% -> 0%
where the time goes in v1:
time: 192 us
  blocking collectives  89.5 us (47%)
  waiting for transfers between devices  64.6 us (34%)
  Pallas kernels  23.1 us (12%)
  starting transfers between devices  7.37 us (4%)
  local copies, waits for them, and re-layouts  5.52 us (3%)
    all_to_all x1, blocking collectives, per_device(): h = lax.all_to_all(outgoing, 'sector', 0, 0, tiled=True)  54.2 us
    all_to_all x1, waiting for transfers between devices, per_device(): arrived = lax.all_to_all(pieces, 'sector', 0, 0, tiled=True)  48.6 us
    all_to_all x1, blocking collectives, per_device(): arrived_parts = lax.all_to_all(parts, 'row', 0, 0, tiled=True)  35.3 us
    ppermute x1, waiting for transfers between devices, per_device(): halo = lax.ppermute(h[:REACH], 'row', backward)  16 us
    pallas_call x1, Pallas kernels, project(): pl.pallas_call(project_kernel, in_specs=[vmem] * 4, out_specs=vmem, out_s...  14.4 us
    pallas_call x1, Pallas kernels, transform(): pl.pallas_call(transform_kernel, grid_spec=spec, out_shape=jax.ShapeDtype...  8.72 us
    all_to_all x1, starting transfers between devices, per_device(): arrived = lax.all_to_all(pieces, 'sector', 0, 0, tiled=True)  6.08 us
    reshape x1, local copies, waits for them, and re-layouts, per_device(): psi_sectors.reshape(sec_dev, sector_count, rows_dev // sector_count, cols)  4.65 us
  transfers between devices with their start and end apart: 2, of which 2 were waited for; matrix products, arithmetic and copies ran while one was open for 0% of the time, Pallas kernels for 0%

profile of v1, /device:TPU:2, one launch (start us, length us, event | category | flops | bytes accessed | tf_op | source)
XLA Modules:
  0.0 191.6 jit_solution(14528125811247081740)
XLA Ops:
  0.6 4.6 %copy.9 = bf16[4,16,128,256]{3,2,0,1:T(8,128)(2,1)} copy(bf16[4,16,128,256]{3,2,1,0:T(8,128)(2,1)} %bitcast.7) | data formatting | bytes 8388608 | tf_op jit(solution)/shard_map/reshape | solution.py:235
  5.3 0.0 copy-start.2
  5.3 6.1 %all-to-all-start = ((bf16[16,4,128,256]{3,2,1,0:T(8,128)(2,1)}), bf16[16,4,128,256]{3,2,1,0:T(8,128)(2,1)}, u32[]{:S(2)}, u32[]{:S(2)}) async-start(bf16[16,4,128,256]{3,2,1,0:T(8,128)(2,1)} %bitcast.5), calls=%async_computation | async-start | bytes 8388608 | tf_op jit(solution)/shard_map/all_to_all | solution.py:237
  11.4 0.0 copy-done.2
  11.4 0.6 select_reduce_fusion.slot_ref
  12.0 48.6 %all-to-all-done.x_ref = bf16[16,4,128,256]{3,2,1,0:T(8,128)(2,1)} async-done(((bf16[16,4,128,256]{3,2,1,0:T(8,128)(2,1)}), bf16[16,4,128,256]{3,2,1,0:T(8,128)(2,1)}, u32[]{:S(2)}, u32[]{:S(2)}) %all-to-all-start) | async-done | bytes 4194336 | tf_op jit(solution)/shard_map/all_to_all | solution.py:237
  60.5 8.7 %transform.1 = bf16[64,128,256]{2,1,0:T(8,128)(2,1)} custom-call(s32[32]{0:T(128)} %select_reduce_fusion.slot_ref, bf16[16,4,128,256]{3,2,1,0:T(8,128)(2,1)} %all-to-all-done.x_ref), custom_call_target="tpu_custom_call" | custom-call | flops 22937600 | bytes 8388608 | tf_op jit(solution)/shard_map/transform/pallas_call | solution.py:138
  69.3 0.0 copy-start
  69.3 54.2 %all_to_all.15.h_ref = bf16[16,4,128,256]{3,2,1,0:T(8,128)(2,1)S(1)} all-to-all(bf16[16,4,128,256]{3,2,1,0:T(8,128)(2,1)} %bitcast.6), channel_id=1, replica_groups=mesh['sector'=16,'row'=8] {'sector'}, dimensions={0} | all-to-all | bytes 8388608 | tf_op jit(solution)/shard_map/all_to_all | solution.py:240
  123.4 0.0 copy-start.1
  123.5 1.3 collective-permute-start
  124.8 16.0 %collective-permute-done.halo_ref = bf16[2,4,128,256]{3,2,1,0:T(8,128)(2,1)S(1)} collective-permute-done((bf16[2,4,128,256]{3,2,1,0:T(8,128)(2,1)S(1)}, bf16[2,4,128,256]{3,2,1,0:T(8,128)(2,1)S(1)}, u32[]{:S(2)}, u32[]{:S(2)}) %collective-permute-start) | collective-permute-done | bytes 524320 | tf_op jit(solution)/shard_map/ppermute | solution.py:244
  140.8 0.0 copy-done.1
  140.8 0.0 copy-done
  140.8 14.4 %project.1 = bf16[8,4,64,512]{3,2,1,0:T(8,128)(2,1)S(1)} custom-call(bf16[16,4,128,256]{3,2,1,0:T(8,128)(2,1)} %copy-done.1, bf16[2,4,128,256]{3,2,1,0:T(8,128)(2,1)S(1)} %collective-permute-done.halo_ref, bf16[16,5,128,128]{3,2,1,0:T(8,128)(2,1)S(1)} %copy-done, bf16[16,5,128,128]{3,2,1,0:T(8,128)(2,1)} %mass_ref.1), custom_call_target="tpu_custom_call" | custom-call | flops 7516192768 | bytes 9961472 | tf_op jit(solution)/shard_map/project/pallas_call | solution.py:210
  155.2 35.3 %all_to_all.16 = bf16[8,4,64,512]{3,2,1,0:T(8,128)(2,1)S(1)} all-to-all(bf16[8,4,64,512]{3,2,1,0:T(8,128)(2,1)S(1)} %project.1), channel_id=1, replica_groups=mesh['sector'=16,'row'=8] {'row'}, dimensions={0} | all-to-all | bytes 4194304 | tf_op jit(solution)/shard_map/all_to_all | solution.py:246
  190.5 0.3 convert_reduce_fusion
  190.8 0.8 fusion
  (1 shorter events, 0.0 us)
Async XLA Ops:
  5.3 6.1 %copy-start.2 = (s32[32]{0:T(128)S(1)}, s32[32]{0:T(128)}, u32[]{:S(2)}) copy-start(s32[32]{0:T(128)} %param.7) | copy-start | bytes 388
  5.3 55.3 %all-to-all-start = ((bf16[16,4,128,256]{3,2,1,0:T(8,128)(2,1)}), bf16[16,4,128,256]{3,2,1,0:T(8,128)(2,1)}, u32[]{:S(2)}, u32[]{:S(2)}) async-start(bf16[16,4,128,256]{3,2,1,0:T(8,128)(2,1)} %bitcast.5), calls=%async_computation | async-start | bytes 8388608 | tf_op jit(solution)/shard_map/all_to_all | solution.py:237
  69.3 71.6 %copy-start = (bf16[16,5,128,128]{3,2,1,0:T(8,128)(2,1)S(1)}, bf16[16,5,128,128]{3,2,1,0:T(8,128)(2,1)}, u32[]{:S(2)}) copy-start(bf16[16,5,128,128]{3,2,1,0:T(8,128)(2,1)} %stiff_ref.1) | copy-start | bytes 7864324
  123.4 17.4 %copy-start.1 = (bf16[16,4,128,256]{3,2,1,0:T(8,128)(2,1)}, bf16[16,4,128,256]{3,2,1,0:T(8,128)(2,1)S(1)}, u32[]{:S(2)}) copy-start(bf16[16,4,128,256]{3,2,1,0:T(8,128)(2,1)S(1)} %all_to_all.15.h_ref) | copy-start | bytes 12582916
  123.5 17.3 %collective-permute-start = (bf16[2,4,128,256]{3,2,1,0:T(8,128)(2,1)S(1)}, bf16[2,4,128,256]{3,2,1,0:T(8,128)(2,1)S(1)}, u32[]{:S(2)}, u32[]{:S(2)}) collective-permute-start(bf16[2,4,128,256]{3,2,1,0:T(8,128)(2,1)S(1)} %slice.12), channel_id=1, source_target_pairs={{1,0},{2,1},{3,2},{4,3},{5,4},{6,5},{7,6},{9,8},{10,9},{11,10},{12... | collective-permute-start | bytes 1572872 | tf_op jit(solution)/shard_map/ppermute | solution.py:244

commit v2 on v1

--- a/solution.py
+++ b/solution.py
@@ -10,7 +10,7 @@
 B = 128
 REACH = 2
 LANES = 256
-STEP_ROWS = 16
+STEP_ROWS = 32
 
 
 def slot_of_harmonic(harmonic_table):
@@ -147,84 +147,111 @@
     )(slots, arrived)
 
 
-def project_kernel(h_ref, halo_ref, stiff_ref, mass_ref, out_ref, y_ref, pt_ref, u_ref):
-    blocks = h_ref.shape[0]
-    slots = h_ref.shape[1] // 2
-
-    def window(refs_rows):
-        return jnp.concatenate(refs_rows, axis=0)
-
-    def band_row(i, h0, h1, h2):
+def band_rows(stiff, mass, h0, h1, h2):
+    lhs = jnp.concatenate(
+        [jnp.concatenate([r[2] * jnp.bfloat16(0.5), r[3], r[4]], axis=1) for r in (stiff, mass)], axis=0
+    )
+    parts = []
+    for c in range(2):
+        rhs = jnp.concatenate([h0[c], h1[c], h2[c]], axis=0)
+        parts.append(jnp.dot(lhs, rhs, preferred_element_type=jnp.float32).astype(jnp.bfloat16))
+    return parts
+
+
+def inner_kernel(h_ref, stiff_ref, mass_ref, u_ref, y_ref, pt_ref):
+    count = pt_ref.shape[0]
+
+    def body(i, carry):
         rows = pl.ds(i * B, B)
-        lhs = jnp.concatenate(
-            [
-                jnp.concatenate([r[i, 2] * jnp.bfloat16(0.5), r[i, 3], r[i, 4]], axis=1)
-                for r in (stiff_ref, mass_ref)
-            ],
-            axis=0,
-        )
-        for c in range(2 * slots):
-            rhs = jnp.concatenate([h0[c], h1[c], h2[c]], axis=0)
-            y = jnp.dot(lhs, rhs, preferred_element_type=jnp.float32).astype(jnp.bfloat16)
-            slot, part = c // 2, c % 2
-            lanes = slice(LANES * part, LANES * part + LANES)
-            lanes_m = slice(LANES * (2 + part), LANES * (2 + part) + LANES)
-            y_ref[slot, rows, lanes] = y[:B]
-            y_ref[slot, rows, lanes_m] = y[B:]
-            pt_ref[slot, i, LANES * part : LANES * part + LANES, :] = h0[c].T
-
-    def body(i, carry):
-        band_row(i, h_ref.at[i], h_ref.at[i + 1], h_ref.at[i + 2])
+        h0, h1, h2 = h_ref.at[i], h_ref.at[i + 1], h_ref.at[i + 2]
+        parts = band_rows(stiff_ref.at[i], mass_ref.at[i], h0, h1, h2)
+        for c in range(2):
+            y_ref[rows, LANES * c : LANES * (c + 1)] = parts[c][:B]
+            y_ref[rows, LANES * (2 + c) : LANES * (3 + c)] = parts[c][B:]
+            pt_ref[i, LANES * c : LANES * (c + 1), :] = h0[c].T
         return carry
 
-    lax.fori_loop(0, blocks - 2, body, 0)
-    band_row(blocks - 2, h_ref.at[blocks - 2], h_ref.at[blocks - 1], halo_ref.at[0])
-    band_row(blocks - 1, h_ref.at[blocks - 1], halo_ref.at[0], halo_ref.at[1])
-
-    for slot in range(slots):
-        p_t = jnp.concatenate([pt_ref[slot, i] for i in range(blocks)], axis=1)
-        for n in range(4):
-            u_ref[slot, :, LANES * n : LANES * n + LANES] = jnp.dot(
-                p_t, y_ref[slot, :, LANES * n : LANES * n + LANES], preferred_element_type=jnp.float32
-            )
-    strips = out_ref.shape[0]
-    high = out_ref.shape[2]
-    for kind in range(2):
-        for slot in range(slots):
-            base = 2 * LANES * kind
-            for q in range(4):
-                direct = u_ref[slot, B * q : B * q + B, base : base + 2 * LANES]
-                mirror = u_ref[slot, :, base + B * q : base + B * q + B].T
-                total = (direct + mirror).astype(jnp.bfloat16)
-                for part in range(B // high):
-                    out_ref[q * (B // high) + part, kind * slots + slot] = total[
-                        part * high : (part + 1) * high
-                    ]
-
-
-def project(h, halo, stiff, mass, strips):
-    blocks, comps, _, cols = h.shape
+    lax.fori_loop(0, count, body, 0)
+    p_t = jnp.concatenate([pt_ref[i] for i in range(count)], axis=1)
+    for n in range(4):
+        lanes = slice(LANES * n, LANES * (n + 1))
+        u_ref[0, :, lanes] = jnp.dot(p_t, y_ref[:, lanes], preferred_element_type=jnp.float32)
+
+
+def project_inner(h, stiff, mass):
+    blocks, comps = h.shape[:2]
     slots = comps // 2
-    wide = 2 * cols
+    count = blocks - REACH
     vmem = pl.BlockSpec(memory_space=pltpu.VMEM)
     return pl.pallas_call(
-        project_kernel,
-        in_specs=[vmem] * 4,
-        out_specs=vmem,
-        out_shape=jax.ShapeDtypeStruct((strips, 2 * slots, wide // strips, wide), jnp.bfloat16),
+        inner_kernel,
+        grid=(slots,),
+        in_specs=[pl.BlockSpec((blocks, 2) + h.shape[2:], lambda s: (0, s, 0, 0)), vmem, vmem],
+        out_specs=pl.BlockSpec((1, 2 * LANES, 4 * LANES), lambda s: (s, 0, 0)),
+        out_shape=jax.ShapeDtypeStruct((slots, 2 * LANES, 4 * LANES), jnp.float32),
         scratch_shapes=[
-            pltpu.VMEM((slots, blocks * B, 2 * wide), jnp.bfloat16),
-            pltpu.VMEM((slots, blocks, wide, B), jnp.bfloat16),
-            pltpu.VMEM((slots, wide, 2 * wide), jnp.float32),
+            pltpu.VMEM((count * B, 4 * LANES), jnp.bfloat16),
+            pltpu.VMEM((count, 2 * LANES, B), jnp.bfloat16),
         ],
-        compiler_params=pltpu.CompilerParams(vmem_limit_bytes=48 * 1024 * 1024),
+        compiler_params=pltpu.CompilerParams(vmem_limit_bytes=28 * 1024 * 1024),
         cost_estimate=pl.CostEstimate(
-            flops=slots * blocks * B * wide * (2 * 2 * 3 * B + 2 * 2 * wide),
-            bytes_accessed=2 * (h.size + halo.size + stiff.size + mass.size),
+            flops=slots * count * B * 2 * LANES * (2 * 2 * 3 * B + 2 * 4 * LANES),
+            bytes_accessed=2 * (h.size + stiff.size + mass.size),
             transcendentals=0,
         ),
-        name="project",
-    )(h, halo, stiff, mass)
+        name="project_inner",
+    )(h, stiff, mass)
+
+
+def last_kernel(h_ref, halo_ref, stiff_ref, mass_ref, u_ref, out_ref, v_ref):
+    rows = [h_ref.at[0], h_ref.at[1], halo_ref.at[0], halo_ref.at[1]]
+    parts = [band_rows(stiff_ref.at[i], mass_ref.at[i], *rows[i : i + 3]) for i in range(2)]
+    p_t = jnp.concatenate(
+        [jnp.concatenate([h_ref[i, c].T for c in range(2)], axis=0) for i in range(2)], axis=1
+    )
+    for n in range(4):
+        kind, c = n // 2, n % 2
+        lanes = slice(LANES * n, LANES * (n + 1))
+        y = jnp.concatenate([parts[i][c][B * kind : B * (kind + 1)] for i in range(2)], axis=0)
+        v_ref[:, lanes] = u_ref[0, :, lanes] + jnp.dot(p_t, y, preferred_element_type=jnp.float32)
+    high = out_ref.shape[3]
+    for kind in range(2):
+        base = 2 * LANES * kind
+        for q in range(4):
+            direct = v_ref[B * q : B * (q + 1), base : base + 2 * LANES]
+            mirror = v_ref[:, base + B * q : base + B * (q + 1)].T
+            total = (direct + mirror).astype(jnp.bfloat16)
+            for part in range(B // high):
+                out_ref[q * (B // high) + part, kind, 0] = total[part * high : (part + 1) * high]
+
+
+def project_last(h, halo, stiff, mass, u, strips):
+    blocks, comps = h.shape[:2]
+    slots = comps // 2
+    at = blocks // REACH - 1
+    high = 2 * LANES // strips
+    ends = lambda s: (at, 0, 0, 0)
+    return pl.pallas_call(
+        last_kernel,
+        grid=(slots,),
+        in_specs=[
+            pl.BlockSpec((REACH, 2) + h.shape[2:], lambda s: (at, s, 0, 0)),
+            pl.BlockSpec((REACH, 2) + h.shape[2:], lambda s: (0, s, 0, 0)),
+            pl.BlockSpec((REACH,) + stiff.shape[1:], ends),
+            pl.BlockSpec((REACH,) + mass.shape[1:], ends),
+            pl.BlockSpec((1,) + u.shape[1:], lambda s: (s, 0, 0)),
+        ],
+        out_specs=pl.BlockSpec((strips, 2, 1, high, 2 * LANES), lambda s: (0, 0, s, 0, 0)),
+        out_shape=jax.ShapeDtypeStruct((strips, 2, slots, high, 2 * LANES), jnp.bfloat16),
+        scratch_shapes=[pltpu.VMEM((2 * LANES, 4 * LANES), jnp.float32)],
+        compiler_params=pltpu.CompilerParams(vmem_limit_bytes=20 * 1024 * 1024),
+        cost_estimate=pl.CostEstimate(
+            flops=slots * REACH * B * 2 * LANES * (2 * 2 * 3 * B + 2 * 4 * LANES),
+            bytes_accessed=4 * u.size + 4 * strips * slots * high * 2 * LANES,
+            transcendentals=0,
+        ),
+        name="project_last",
+    )(h, halo, stiff, mass, u)
 
 
 def per_device(psi_sectors, stiff_blocks, mass_blocks, harmonic_table):
@@ -242,11 +269,11 @@
     h = jnp.swapaxes(h, 1, 2).reshape(blocks, sec_dev, B, cols)
     backward = [(i + 1, i) for i in range(row_count - 1)]
     halo = lax.ppermute(h[:REACH], "row", backward)
-    parts = project(h, halo, stiff_blocks, mass_blocks, row_count)
+    u = project_inner(h, stiff_blocks, mass_blocks)
+    parts = project_last(h, halo, stiff_blocks, mass_blocks, u, row_count)
     arrived_parts = lax.all_to_all(parts, "row", 0, 0, tiled=True)
     total = jnp.sum(arrived_parts.astype(jnp.float32), axis=0)
-    slots = sec_dev // 2
-    return total[:slots], total[slots:]
+    return total[0], total[1]
 
 
 def solution(mesh):

time: 192 us -> 179 us (0.932)
  waiting for transfers between devices: 64.6 us -> 51.7 us
    ppermute x1, waiting for transfers between devices: 16 us -> 3.08 us  [per_device(): halo = lax.ppermute(h[:REACH], 'row', backward)]
    pallas_call x1 -> x2, Pallas kernels: 14.4 us -> 15.5 us  [the longest x1 12.9 us: project_inner(): pl.pallas_call(inner_kernel, grid=(slots,), in_specs=[pl.BlockSpec((block...]
  transfers between devices with their start and end apart: 2 -> 2, of which waited for: 2 -> 2; matrix products, arithmetic and copies ran while one was open for 0% -> 0% of each run, Pallas kernels for 0% -> 7%
where the time goes in v2:
time: 179 us; the launch traced here: 178 us
  blocking collectives  89.6 us (50%)
  waiting for transfers between devices  51.7 us (29%)
  Pallas kernels  22.7 us (13%)
  starting transfers between devices  7.37 us (4%)
  local copies, waits for them, and re-layouts  5.52 us (3%)
    all_to_all x1, blocking collectives, per_device(): h = lax.all_to_all(outgoing, 'sector', 0, 0, tiled=True)  54.3 us
    all_to_all x1, waiting for transfers between devices, per_device(): arrived = lax.all_to_all(pieces, 'sector', 0, 0, tiled=True)  48.6 us
    all_to_all x1, blocking collectives, per_device(): arrived_parts = lax.all_to_all(parts, 'row', 0, 0, tiled=True)  35.3 us
    pallas_call x1, Pallas kernels, project_inner(): pl.pallas_call(inner_kernel, grid=(slots,), in_specs=[pl.BlockSpec((block...  12.9 us
    pallas_call x1, Pallas kernels, transform(): pl.pallas_call(transform_kernel, grid_spec=spec, out_shape=jax.ShapeDtype...  7.22 us
    all_to_all x1, starting transfers between devices, per_device(): arrived = lax.all_to_all(pieces, 'sector', 0, 0, tiled=True)  6.08 us
    reshape x1, local copies, waits for them, and re-layouts, per_device(): psi_sectors.reshape(sec_dev, sector_count, rows_dev // sector_count, cols)  4.65 us
  transfers between devices with their start and end apart: 2, of which 2 were waited for; matrix products, arithmetic and copies ran while one was open for 0% of the time, Pallas kernels for 7%

profile of v2, /device:TPU:2, one launch (start us, length us, event | category | flops | bytes accessed | tf_op | source)
XLA Modules:
  0.0 178.4 jit_solution(16645953696460489177)
XLA Ops:
  0.6 4.6 %copy.9 = bf16[4,16,128,256]{3,2,0,1:T(8,128)(2,1)} copy(bf16[4,16,128,256]{3,2,1,0:T(8,128)(2,1)} %bitcast.11) | data formatting | bytes 8388608 | tf_op jit(solution)/shard_map/reshape | solution.py:262
  5.3 0.0 copy-start.2
  5.3 6.1 %all-to-all-start = ((bf16[16,4,128,256]{3,2,1,0:T(8,128)(2,1)}), bf16[16,4,128,256]{3,2,1,0:T(8,128)(2,1)}, u32[]{:S(2)}, u32[]{:S(2)}) async-start(bf16[16,4,128,256]{3,2,1,0:T(8,128)(2,1)} %bitcast.9), calls=%async_computation | async-start | bytes 8388608 | tf_op jit(solution)/shard_map/all_to_all | solution.py:264
  11.4 0.0 copy-done.2
  11.4 0.6 select_reduce_fusion.slot_ref
  12.0 48.6 %all-to-all-done.x_ref = bf16[16,4,128,256]{3,2,1,0:T(8,128)(2,1)} async-done(((bf16[16,4,128,256]{3,2,1,0:T(8,128)(2,1)}), bf16[16,4,128,256]{3,2,1,0:T(8,128)(2,1)}, u32[]{:S(2)}, u32[]{:S(2)}) %all-to-all-start) | async-done | bytes 4194336 | tf_op jit(solution)/shard_map/all_to_all | solution.py:264
  60.5 7.2 %transform.1 = bf16[64,128,256]{2,1,0:T(8,128)(2,1)} custom-call(s32[32]{0:T(128)} %select_reduce_fusion.slot_ref, bf16[16,4,128,256]{3,2,1,0:T(8,128)(2,1)} %all-to-all-done.x_ref), custom_call_target="tpu_custom_call" | custom-call | flops 22937600 | bytes 8388608 | tf_op jit(solution)/shard_map/transform/pallas_call | solution.py:138
  67.8 0.0 copy-start
  67.8 0.0 copy-start.1
  67.8 54.3 %all_to_all.15.h_ref = bf16[16,4,128,256]{3,2,1,0:T(8,128)(2,1)S(1)} all-to-all(bf16[16,4,128,256]{3,2,1,0:T(8,128)(2,1)} %bitcast.10), channel_id=1, replica_groups=mesh['sector'=16,'row'=8] {'sector'}, dimensions={0} | all-to-all | bytes 8388608 | tf_op jit(solution)/shard_map/all_to_all | solution.py:267
  122.1 1.3 collective-permute-start
  123.4 0.0 copy-done
  123.4 0.0 copy-done.1
  123.4 12.9 %project_inner.1.u_ref = f32[2,512,1024]{2,1,0:T(8,128)S(1)} custom-call(bf16[16,4,128,256]{3,2,1,0:T(8,128)(2,1)S(1)} %all_to_all.15.h_ref, bf16[16,5,128,128]{3,2,1,0:T(8,128)(2,1)S(1)} %copy-done, bf16[16,5,128,128]{3,2,1,0:T(8,128)(2,1)S(1)} %copy-done.1), custom_call_target="tpu_custom_call" | custom-call | flops 6576668672 | bytes 9437184 | tf_op jit(solution)/shard_map/project_inner/pallas_call | solution.py:186
  136.4 3.1 %collective-permute-done.halo_ref = bf16[2,4,128,256]{3,2,1,0:T(8,128)(2,1)S(1)} collective-permute-done((bf16[2,4,128,256]{3,2,1,0:T(8,128)(2,1)S(1)}, bf16[2,4,128,256]{3,2,1,0:T(8,128)(2,1)S(1)}, u32[]{:S(2)}, u32[]{:S(2)}) %collective-permute-start) | collective-permute-done | bytes 524320 | tf_op jit(solution)/shard_map/ppermute | solution.py:271
  139.5 2.6 %project_last.1 = bf16[8,2,2,64,512]{4,3,2,1,0:T(8,128)(2,1)S(1)} custom-call(bf16[16,4,128,256]{3,2,1,0:T(8,128)(2,1)S(1)} %all_to_all.15.h_ref, bf16[2,4,128,256]{3,2,1,0:T(8,128)(2,1)S(1)} %collective-permute-done.halo_ref, bf16[16,5,128,128]{3,2,1,0:T(8,128)(2,1)S(1)} %copy-done, bf16[16,5,128,128]{3,2,1,0:T(8,128)(2,1)S(1)} %copy-done.1, ...), custom_call_target="tpu_custom_call" | custom-call | flops 939524096 | bytes 6291456 | tf_op jit(solution)/shard_map/project_last/pallas_call | solution.py:234
  142.0 35.3 %all_to_all.16 = bf16[8,2,2,64,512]{4,3,2,1,0:T(8,128)(2,1)S(1)} all-to-all(bf16[8,2,2,64,512]{4,3,2,1,0:T(8,128)(2,1)S(1)} %project_last.1), channel_id=1, replica_groups=mesh['sector'=16,'row'=8] {'row'}, dimensions={0} | all-to-all | bytes 4194304 | tf_op jit(solution)/shard_map/all_to_all | solution.py:274
  177.3 0.3 convert_reduce_fusion
  177.6 0.8 slice_bitcast_fusion
  (1 shorter events, 0.0 us)
Async XLA Ops:
  5.3 6.1 %copy-start.2 = (s32[32]{0:T(128)S(1)}, s32[32]{0:T(128)}, u32[]{:S(2)}) copy-start(s32[32]{0:T(128)} %param.7) | copy-start | bytes 388
  5.3 55.3 %all-to-all-start = ((bf16[16,4,128,256]{3,2,1,0:T(8,128)(2,1)}), bf16[16,4,128,256]{3,2,1,0:T(8,128)(2,1)}, u32[]{:S(2)}, u32[]{:S(2)}) async-start(bf16[16,4,128,256]{3,2,1,0:T(8,128)(2,1)} %bitcast.9), calls=%async_computation | async-start | bytes 8388608 | tf_op jit(solution)/shard_map/all_to_all | solution.py:264
  67.8 55.7 %copy-start = (bf16[16,5,128,128]{3,2,1,0:T(8,128)(2,1)S(1)}, bf16[16,5,128,128]{3,2,1,0:T(8,128)(2,1)}, u32[]{:S(2)}) copy-start(bf16[16,5,128,128]{3,2,1,0:T(8,128)(2,1)} %stiff_ref.3) | copy-start | bytes 7864324
  67.8 55.7 %copy-start.1 = (bf16[16,5,128,128]{3,2,1,0:T(8,128)(2,1)S(1)}, bf16[16,5,128,128]{3,2,1,0:T(8,128)(2,1)}, u32[]{:S(2)}) copy-start(bf16[16,5,128,128]{3,2,1,0:T(8,128)(2,1)} %mass_ref.3) | copy-start | bytes 7864324
  122.1 17.3 %collective-permute-start = (bf16[2,4,128,256]{3,2,1,0:T(8,128)(2,1)S(1)}, bf16[2,4,128,256]{3,2,1,0:T(8,128)(2,1)S(1)}, u32[]{:S(2)}, u32[]{:S(2)}) collective-permute-start(bf16[2,4,128,256]{3,2,1,0:T(8,128)(2,1)S(1)} %slice.12), channel_id=1, source_target_pairs={{1,0},{2,1},{3,2},{4,3},{5,4},{6,5},{7,6},{9,8},{10,9},{11,10},{12... | collective-permute-start | bytes 1572872 | tf_op jit(solution)/shard_map/ppermute | solution.py:271
